TPU v7x, 32 devices: a whole 2x2x4 slice. The times are simulated.
32 devices in a mesh: rows: 2 (over core), cols: 4 (over y, x), slabs: 4 (over z).
Axes of the slice: x: 2, y: 2, z: 4, core: 2. Of those that a mesh axis runs over, the one named last changes fastest.
Arguments:
- tracer: float32 [8, 256, 384, 128], P('rows', 'cols', 'slabs'), may hold values from 0.2 to 1.8
- crowding: float32 [8, 256, 384, 128], P('rows', 'cols', 'slabs'), may hold values from 0.5 to 2
Outputs:
- tracer_end: float32 [8, 256, 384, 128], P('rows', 'cols', 'slabs')
All inputs are finite; a program needn't handle non-finite values.
Results may differ from a plain program's by a relative error of at most 0.00002.
Values sent between devices are 32-bit elements.
A program may use at most 448 MiB of HBM per device.

v0:
```python
import functools

import jax
import jax.numpy as jnp
from jax import lax
from jax.experimental import pallas as pl
from jax.experimental.pallas import tpu as pltpu
from jax.sharding import PartitionSpec as P

STEPS = 4
EDGE = 2
VIA = {1: 3, 2: 0}
GAP = 1
LATE = 3
RELAYED = 1
MIDDLE = 10
PAD = 8
VMEM_LIMIT = 40 * 1024 * 1024
MESH = pl.DeviceIdType.MESH
AXES = ("rows", "cols", "slabs")


class Levels:
    def __init__(self, *refs):
        self.refs = refs

    @property
    def at(self):
        return self

    def __getitem__(self, index):
        return self.refs[index[0]].at[index[1:]]


def write(ended, out, store_sem):
    rows, width, depth, species = out.shape
    copies = [pltpu.make_async_copy(
        ended.at[1 + y, pl.ds(1, width), pl.ds(PAD, depth)], out.at[y], store_sem.at[y])
        for y in range(rows)]
    for copy in copies:
        copy.start()
    for copy in copies:
        copy.wait()


def kernel(sizes, chunks, via, tracer, crowding, ended, other_field, limit, load_sem,
           y_send, y_recv, z_send, z_recv, x_send, x_recv,
           relayed, r_send, r_recv, f_send, f_recv):
    rows, width, depth, species = tracer.shape
    last = chunks - 1
    field = Levels(ended, other_field)
    place = {axis: lax.axis_index(axis) for axis in AXES}
    has = {(axis, side): (place[axis] > 0) if side == 0 else (place[axis] < sizes[axis] - 1)
           for axis in AXES for side in (0, 1)}
    near = {(axis, side): {axis: jnp.clip(place[axis] + 2 * side - 1, 0, sizes[axis] - 1)}
            for axis in AXES for side in (0, 1)}

    col = place["cols"]
    direct = rows - min(RELAYED, rows // 2) if via else rows

    def span(k):
        if isinstance(k, int):
            if k == 0:
                return 0, EDGE
            if k == last:
                return width - EDGE, EDGE
        return EDGE + (k - 1) * MIDDLE, MIDDLE

    def face(axis, side, p, k, from_input, to, part=rows):
        start, count = span(k)
        at, cells = pl.ds(PAD, depth), pl.ds(1 + start, count)
        other = 1 - side
        if axis == "rows":
            src = (tracer.at[side * (rows - 1), pl.ds(start, count)] if from_input
                   else field.at[p, 1 + side * (rows - 1), cells, at])
            dst = field.at[p, other * (rows + 1), cells, at]
            send, recv = y_send.at[p, side, k], y_recv.at[p, other, k]
        elif axis == "slabs":
            src = (tracer.at[:, pl.ds(start, count), pl.ds(side * (depth - 1), 1)] if from_input
                   else field.at[p, pl.ds(1, rows), cells, pl.ds(PAD + side * (depth - 1), 1)])
            dst = field.at[p, pl.ds(1, rows), cells, pl.ds(PAD - 1 + other * (depth + 1), 1)]
            send, recv = z_send.at[p, side, k], z_recv.at[p, other, k]
        else:
            src = (tracer.at[pl.ds(0, part), side * (width - 1)] if from_input
                   else field.at[p, pl.ds(1, part), 1 + side * (width - 1), at])
            dst = field.at[p, pl.ds(1, part), other * (width + 1), at]
            send, recv = x_send.at[p, side], x_recv.at[p, other]
        return pltpu.make_async_remote_copy(
            src_ref=src, dst_ref=dst, send_sem=send, recv_sem=recv,
            device_id=near[axis, to], device_id_type=MESH)

    def x_face(side, to, p, from_input, action):
        if not via:
            pl.when(has["cols", to])(lambda: action(face("cols", side, p, 0, from_input, to)))
            return
        long = col == 2 - to
        pl.when(long)(lambda: action(face("cols", side, p, 0, from_input, to, direct)))
        pl.when(jnp.logical_and(has["cols", to], jnp.logical_not(long)))(
            lambda: action(face("cols", side, p, 0, from_input, to)))

    def first_hop(source, event, row, from_input):
        side = 2 - source
        src = (tracer.at[direct + row, side * (width - 1)] if from_input
               else field.at[event % 2, 1 + direct + row, 1 + side * (width - 1), pl.ds(PAD, depth)])
        return pltpu.make_async_remote_copy(
            src_ref=src, dst_ref=relayed.at[event, row],
            send_sem=r_send.at[event, row], recv_sem=r_recv.at[event, row],
            device_id={"cols": via[source]}, device_id_type=MESH)

    def second_hop(source, event, row):
        side = 2 - source
        return pltpu.make_async_remote_copy(
            src_ref=relayed.at[event, row],
            dst_ref=field.at[event % 2, 1 + direct + row, (1 - side) * (width + 1), pl.ds(PAD, depth)],
            send_sem=f_send.at[event, row], recv_sem=f_recv.at[event, row],
            device_id={"cols": 3 - source}, device_id_type=MESH)

    def hops(action, *who):
        if via:
            for source in (1, 2):
                @pl.when(col == who[source - 1])
                def _():
                    for row in range(rows - direct):
                        action(source, row)

    def in_order(action):
        def both(*sides):
            for side in sides:
                action(side)

        if via:
            pl.when(col == 1)(lambda: both(1, 0))
            pl.when(col != 1)(lambda: both(0, 1))
        else:
            both(0, 1)

    def pass_on(event, row):
        for source in (1, 2):
            @pl.when(col == via[source])
            def _():
                first_hop(source, event, row, False).wait_recv()
                second_hop(source, event, row).start()

    def each(axes, action):
        for axis in axes:
            for side in (0, 1):
                pl.when(has[axis, side])(functools.partial(action, axis, side))

    def send(axes, p, k, from_input=False):
        each(axes, lambda axis, side: face(axis, side, p, k, from_input, side).start())

    def sent(axes, p, k):
        each(axes, lambda axis, side: face(axis, side, p, k, False, side).wait_send())

    def received(axes, p, k):
        each(axes, lambda axis, side: face(axis, 1 - side, p, k, False, side).wait_recv())

    def load(which, k):
        start, count = span(k)
        if which == 0:
            return pltpu.make_async_copy(
                tracer.at[:, pl.ds(start, count)],
                field.at[0, pl.ds(1, rows), pl.ds(1 + start, count), pl.ds(PAD, depth)],
                load_sem.at[0, k])
        return pltpu.make_async_copy(
            crowding.at[:, pl.ds(start, count)], limit.at[:, pl.ds(start, count)], load_sem.at[1, k])

    barrier = pltpu.get_barrier_semaphore()
    each(AXES, lambda axis, side: pl.semaphore_signal(
        barrier, inc=1, device_id=near[axis, side], device_id_type=MESH))
    for k in range(chunks):
        load(0, k).start()
        load(1, k).start()
    if via:
        pl.semaphore_signal(barrier, inc=1, device_id={"cols": lax.rem(col + 2, 4)}, device_id_type=MESH)
    pl.semaphore_wait(barrier, (1 if via else 0) + sum(jnp.where(has[key], 1, 0) for key in has))

    hops(lambda source, row: first_hop(source, 0, row, True).start(), 1, 2)
    in_order(lambda side: x_face(side, side, 0, True, lambda copy: copy.start()))
    for k in [*range(1, last), 0, last]:
        send(("rows", "slabs"), 0, k, True)

    def clear(axis, side):
        @pl.when(jnp.logical_not(has[axis, side]))
        def _():
            for p in (0, 1):
                if axis == "rows":
                    @pl.loop(1, width + 1)
                    def _(x):
                        field.refs[p][side * (rows + 1), x, pl.ds(PAD, depth)] = jnp.zeros((depth, species), jnp.float32)
                elif axis == "cols":
                    @pl.loop(1, rows + 1)
                    def _(y):
                        field.refs[p][y, side * (width + 1), pl.ds(PAD, depth)] = jnp.zeros((depth, species), jnp.float32)
                else:
                    @pl.loop(1, width + 1)
                    def _(x):
                        for y in range(1, rows + 1):
                            field.refs[p][y, x, pl.ds(PAD - 1 + side * (depth + 1), 1)] = jnp.zeros((1, species), jnp.float32)

    for axis in AXES:
        for side in (0, 1):
            clear(axis, side)

    def advance(step, k):
        p = step % 2
        start, count = span(k)
        scale = 0.2 if step == 0 else 0.05 if step == STEPS - 1 else 0.1

        @pl.loop(0, depth // 8)
        def _(tile):
            at = pl.multiple_of(PAD + tile * 8, 8)
            source = pl.multiple_of(tile * 8, 8)

            def cell(y, x, shift=0):
                return field.refs[p][y, 1 + start + x, pl.ds(at + shift, 8)]

            before = [cell(y, -1) for y in range(1, rows + 1)]
            here = [cell(y, 0) for y in range(1, rows + 1)]
            for x in range(count):
                after = [cell(y, x + 1) for y in range(1, rows + 1)]
                column = [cell(0, x), *here, cell(rows + 1, x)]
                for y in range(rows):
                    middle = here[y]
                    around = (before[y] + after[y]) + (column[y] + column[y + 2])
                    around = around + (cell(y + 1, x, -1) + cell(y + 1, x, 1))
                    bound = limit[y, start + x, pl.ds(source, 8)]
                    if step == 0:
                        bound = bound + bound
                    field.refs[1 - p][y + 1, 1 + start + x, pl.ds(at, 8)] = scale * (around + middle * (6.0 - bound * middle))
                before, here = here, after

    def chunk(step, k, edge):
        p = step % 2
        axes = AXES if edge else ("rows", "slabs")
        if step == 0:
            load(1, k).wait()
            if not edge:
                pl.when(k < last - 1)(lambda: load(0, k + 1).wait())
                pl.when(k == last - 1)(lambda: load(0, last).wait())
        both = ("rows", "slabs")
        received(both, p, k)
        if step >= 1:
            sent(both, 1 - p, k)
        if edge:
            side = 0 if k == 0 else 1
            x_face(1 - side, side, p, False, lambda copy: copy.wait_recv())
            if via:
                @pl.when(col == 2 - side)
                def _():
                    for row in range(rows - direct):
                        second_hop(1 + side, step, row).wait_recv()
            if step >= 1:
                x_face(side, side, 1 - p, False, lambda copy: copy.wait_send())
                if via:
                    @pl.when(col == 2 - side)
                    def _():
                        for row in range(rows - direct):
                            first_hop(2 - side, step - 1, row, False).wait_send()
        advance(step, k)
        if step < STEPS - 1:
            if edge:
                if via:
                    @pl.when(col == 2 - side)
                    def _():
                        for row in range(rows - direct):
                            first_hop(2 - side, step + 1, row, False).start()
                x_face(side, side, 1 - p, False, lambda copy: copy.start())
            send(both, 1 - p, k)

    for step in range(STEPS):
        if step == 0:
            load(0, 0).wait()
            load(0, 1).wait()

        @pl.loop(1, last)
        def _(k):
            chunk(step, k, False)
            if via:
                for row in range(rows - direct):
                    pl.when(k == max(1, last - 1 - LATE - GAP * (rows - direct - 1 - row)))(
                        functools.partial(pass_on, step, row))

        in_order(lambda side: chunk(step, side * last, True))

    p = (STEPS - 1) % 2

    @pl.loop(1, last)
    def _(k):
        sent(("rows", "slabs"), p, k)

    for k in (0, last):
        sent(("rows", "slabs"), p, k)
    for side in (0, 1):
        x_face(side, side, p, False, lambda copy: copy.wait_send())
    hops(lambda source, row: first_hop(source, STEPS - 1, row, False).wait_send(), 1, 2)
    for event in range(STEPS):
        hops(lambda source, row: second_hop(source, event, row).wait_send(), *[via[k] for k in (1, 2)] if via else ())


def relays(mesh):
    if mesh.shape["cols"] != 4:
        return None
    devices = mesh.devices.transpose([mesh.axis_names.index(axis) for axis in AXES])[0, :, 0]
    chips = [getattr(device, "coords", None) for device in devices]
    if any(chip is None for chip in chips):
        return None
    apart = sum(a != b for a, b in zip(chips[1], chips[2]))
    return VIA if apart > 1 else None


def solution(mesh):
    sizes = dict(mesh.shape)
    via = relays(mesh)

    def on_device(tracer, crowding):
        rows, width, depth, species = tracer.shape
        chunks = (width - 2 * EDGE) // MIDDLE + 2
        dma = pltpu.SemaphoreType.DMA
        padded = (rows + 2, width + 2, depth + 2 * PAD, species)
        cell_count = rows * width * depth * species
        ended = pl.pallas_call(
            functools.partial(kernel, sizes, chunks, via),
            out_shape=pltpu.VMEM(padded, jnp.float32),
            in_specs=[pl.BlockSpec(memory_space=pl.ANY)] * 2,
            out_specs=pl.BlockSpec(memory_space=pltpu.VMEM),
            scratch_shapes=[
                pltpu.VMEM(padded, jnp.float32),
                pltpu.VMEM(tracer.shape, jnp.float32),
                dma((2, chunks)),
                dma((2, 2, chunks)), dma((2, 2, chunks)),
                dma((2, 2, chunks)), dma((2, 2, chunks)),
                dma((2, 2)), dma((2, 2)),
                pltpu.VMEM((STEPS, max(1, rows // 2), depth, species), jnp.float32),
                *[dma((STEPS, max(1, rows // 2)))] * 4,
            ],
            compiler_params=pltpu.CompilerParams(
                collective_id=0, has_side_effects=True, vmem_limit_bytes=VMEM_LIMIT),
        )(tracer, crowding)
        return pl.pallas_call(
            write,
            out_shape=jax.ShapeDtypeStruct(tracer.shape, jnp.float32),
            in_specs=[pl.BlockSpec(memory_space=pltpu.VMEM)],
            out_specs=pl.BlockSpec(memory_space=pl.ANY),
            scratch_shapes=[dma((rows,))],
            compiler_params=pltpu.CompilerParams(vmem_limit_bytes=1 << 20),
        )(ended)

    return jax.shard_map(
        on_device, mesh=mesh,
        in_specs=(P("rows", "cols", "slabs", None), P("rows", "cols", "slabs", None)),
        out_specs=P("rows", "cols", "slabs", None), check_vma=False)
```

profile of v0, /device:TPU:0, one launch (start us, length us, event | category | flops | bytes accessed | tf_op | source)
XLA Modules:
  0.0 42.1 jit_solution(4809154029340356588)
XLA Ops:
  0.0 37.4 %shard_map.28.ended = f32[6,66,112,128]{3,2,1,0:T(8,128)S(1)} custom-call(f32[4,64,96,128]{3,2,1,0:T(8,128)} %tracer.1, f32[4,64,96,128]{3,2,1,0:T(8,128)} %crowding.1), custom_call_target="tpu_custom_call" | custom-call | tf_op jit(solution)/shard_map/pallas_call | solution.py:322
  37.4 4.7 %shard_map.29 = f32[4,64,96,128]{3,2,1,0:T(8,128)} custom-call(f32[6,66,112,128]{3,2,1,0:T(8,128)S(1)} %shard_map.28.ended), custom_call_target="tpu_custom_call" | custom-call | tf_op jit(solution)/shard_map/pallas_call | solution.py:340
where the time goes:
time: 42.3 us; the launch traced here: 42.1 us
  Pallas kernels  42.1 us (100%)
    pallas_call x1, Pallas kernels, on_device(): pl.pallas_call(functools.partial(kernel, sizes, chunks, via), out_shape=p...  37.4 us
    pallas_call x1, Pallas kernels, on_device(): pl.pallas_call(write, out_shape=jax.ShapeDtypeStruct(tracer.shape, jnp.fl...  4.72 us

commit v1 on v0

v1 whole, which is shorter than its diff:
```python
import functools

import jax
import jax.numpy as jnp
from jax import lax
from jax.experimental import pallas as pl
from jax.experimental.pallas import tpu as pltpu
from jax.sharding import PartitionSpec as P

STEPS = 4
EDGE = 2
VIA = {1: 3, 2: 0}
LATE = 2
FIRST = 0
PAD = 8
VMEM_LIMIT = 40 * 1024 * 1024
MESH = pl.DeviceIdType.MESH
AXES = ("rows", "cols", "slabs")


def write(ended, out, store_sem):
    rows, width, depth, species = out.shape
    copies = [pltpu.make_async_copy(
        ended.at[1 + y, pl.ds(1, width), pl.ds(PAD, depth)], out.at[y], store_sem.at[y])
        for y in range(rows)]
    for copy in copies:
        copy.start()
    for copy in copies:
        copy.wait()


def kernel(sizes, via, tracer, crowding, ended, other_field, limit, load_sem,
           y_send, y_recv, z_send, z_recv, e_send, e_recv, x_send, x_recv,
           relayed, r_recv, f_send):
    rows, width, depth, species = tracer.shape
    slots = rows
    middle = (width - 2 * EDGE) // slots
    last = slots + 1
    half = rows // 2 if rows % 2 == 0 else rows
    share = rows // 2
    field = (ended, other_field)
    place = {axis: lax.axis_index(axis) for axis in AXES}
    has = {(axis, side): (place[axis] > 0) if side == 0 else (place[axis] < sizes[axis] - 1)
           for axis in AXES for side in (0, 1)}
    near = {(axis, side): {axis: jnp.clip(place[axis] + 2 * side - 1, 0, sizes[axis] - 1)}
            for axis in AXES for side in (0, 1)}
    col = place["cols"]
    upward = lax.rem(place["rows"], 2) == 1
    inner = pl.ds(PAD, depth)

    def row(j):
        return jnp.where(upward, j, rows - 1 - j)

    def span(k):
        if isinstance(k, int):
            if k == 0:
                return 0, EDGE
            if k == last:
                return width - EDGE, EDGE
        return EDGE + (k - 1) * middle, middle

    def remote(axis, to, src, dst, send, recv):
        return pltpu.make_async_remote_copy(
            src_ref=src, dst_ref=dst, send_sem=send, recv_sem=recv,
            device_id=near[axis, to], device_id_type=MESH)

    def y_face(side, p, k, from_input, to):
        start, count = span(k)
        cells, other = pl.ds(1 + start, count), 1 - side
        src = (tracer.at[side * (rows - 1), pl.ds(start, count)] if from_input
               else field[p].at[1 + side * (rows - 1), cells, inner])
        return remote("rows", to, src, field[p].at[other * (rows + 1), cells, inner],
                      y_send.at[p, side, k], y_recv.at[p, other, k])

    def z_face(side, p, k, from_input, to):
        start, count = span(k)
        cells, other, ys = pl.ds(1 + start, count), 1 - side, pl.ds(1, rows)
        src = (tracer.at[:, pl.ds(start, count), pl.ds(side * (depth - 1), 1)] if from_input
               else field[p].at[ys, cells, pl.ds(PAD + side * (depth - 1), 1)])
        return remote("slabs", to, src, field[p].at[ys, cells, pl.ds(PAD - 1 + other * (depth + 1), 1)],
                      z_send.at[p, side, k], z_recv.at[p, other, k])

    def e_face(side, p, edge, group, from_input, to):
        start, count = span(edge * last)
        cells, other = pl.ds(1 + start, count), 1 - side
        first = jnp.where(upward, group * half, rows - (group + 1) * half)
        src = (tracer.at[pl.ds(first, half), pl.ds(start, count), pl.ds(side * (depth - 1), 1)] if from_input
               else field[p].at[pl.ds(1 + first, half), cells, pl.ds(PAD + side * (depth - 1), 1)])
        dst = field[p].at[pl.ds(1 + first, half), cells, pl.ds(PAD - 1 + other * (depth + 1), 1)]
        return remote("slabs", to, src, dst, e_send.at[p, side, edge, group], e_recv.at[p, other, edge, group])

    def x_source(side, event, j, from_input):
        return (tracer.at[row(j), side * (width - 1)] if from_input
                else field[event % 2].at[1 + row(j), 1 + side * (width - 1), inner])

    def x_face(side, event, j, from_input, to):
        p, other = event % 2, 1 - side
        return remote("cols", to, x_source(side, event, j, from_input),
                      field[p].at[1 + row(j), other * (width + 1), inner],
                      x_send.at[p, side, j], x_recv.at[p, other, j])

    def first_relayed(event):
        return 0 if event % 2 == 0 else rows - share

    def first_hop(source, event, j, from_input):
        side, n = 2 - source, j - first_relayed(event)
        return pltpu.make_async_remote_copy(
            src_ref=x_source(side, event, j, from_input), dst_ref=relayed.at[event, n],
            send_sem=x_send.at[event % 2, side, j], recv_sem=r_recv.at[event, n],
            device_id={"cols": via[source]}, device_id_type=MESH)

    def second_hop(source, event, j):
        side, n, p = 2 - source, j - first_relayed(event), event % 2
        return pltpu.make_async_remote_copy(
            src_ref=relayed.at[event, n],
            dst_ref=field[p].at[1 + row(j), (1 - side) * (width + 1), inner],
            send_sem=f_send.at[event, n], recv_sem=x_recv.at[p, 1 - side, j],
            device_id={"cols": 3 - source}, device_id_type=MESH)

    def send_x(side, event, j, from_input=False):
        if not via:
            pl.when(has["cols", side])(lambda: x_face(side, event, j, from_input, side).start())
            return
        first = first_relayed(event)
        relay = jnp.logical_and(col == 2 - side, jnp.logical_and(j >= first, j < first + share))
        pl.when(relay)(lambda: first_hop(2 - side, event, j, from_input).start())
        pl.when(jnp.logical_and(has["cols", side], jnp.logical_not(relay)))(
            lambda: x_face(side, event, j, from_input, side).start())

    def forward(event, j):
        for source in (1, 2):
            @pl.when(col == via[source])
            def _():
                n = j - first_relayed(event)
                pltpu.make_async_remote_copy(
                    src_ref=relayed.at[event, n], dst_ref=relayed.at[event, n],
                    send_sem=f_send.at[event, n], recv_sem=r_recv.at[event, n],
                    device_id={"cols": 3 - source}, device_id_type=MESH).wait_recv()
                second_hop(source, event, j).start()

    def by_side(axis, action):
        for side in (0, 1):
            pl.when(has[axis, side])(functools.partial(action, side))

    tracer_parts = [(0, EDGE + 1)]
    tracer_parts += [(EDGE + k * middle + 1, middle) for k in range(slots - 1)]
    tracer_parts += [(EDGE + (slots - 1) * middle + 1, middle - 2), (width - EDGE - 1, EDGE + 1)]

    def load_tracer(k):
        start, count = tracer_parts[k]
        return pltpu.make_async_copy(
            tracer.at[:, pl.ds(start, count)],
            field[0].at[pl.ds(1, rows), pl.ds(1 + start, count), inner], load_sem.at[0, k])

    def load_limit(k):
        start, count = span(k)
        return pltpu.make_async_copy(
            crowding.at[:, pl.ds(start, count)], limit.at[:, pl.ds(start, count)], load_sem.at[1, k])

    barrier = pltpu.get_barrier_semaphore()
    for axis in AXES:
        by_side(axis, lambda side: pl.semaphore_signal(
            barrier, inc=1, device_id=near[axis, side], device_id_type=MESH))
    if via:
        pl.semaphore_signal(barrier, inc=1, device_id={"cols": lax.rem(col + 2, 4)}, device_id_type=MESH)
    for k in (0, last, 1):
        load_tracer(k).start()
    for k in (1, 0, last):
        load_limit(k).start()
    for k in range(2, last):
        load_tracer(k).start()
        load_limit(k).start()
    pl.semaphore_wait(barrier, (1 if via else 0) + sum(jnp.where(has[key], 1, 0) for key in has))

    for j in range(rows):
        for side in (0, 1):
            send_x(side, 0, j, True)
    for k in [1, 0, last, *range(2, last)]:
        by_side("rows", lambda side: y_face(side, 0, k, True, side).start())
        if k in (0, last):
            for group in range(rows // half):
                by_side("slabs", lambda side: e_face(side, 0, k // last, group, True, side).start())
        else:
            by_side("slabs", lambda side: z_face(side, 0, k, True, side).start())

    def clear(axis, side):
        @pl.when(jnp.logical_not(has[axis, side]))
        def _():
            for p in (0, 1):
                if axis == "rows":
                    @pl.loop(1, width + 1)
                    def _(x):
                        field[p][side * (rows + 1), x, inner] = jnp.zeros((depth, species), jnp.float32)
                elif axis == "cols":
                    @pl.loop(1, rows + 1)
                    def _(y):
                        field[p][y, side * (width + 1), inner] = jnp.zeros((depth, species), jnp.float32)
                else:
                    @pl.loop(1, width + 1)
                    def _(x):
                        for y in range(1, rows + 1):
                            field[p][y, x, pl.ds(PAD - 1 + side * (depth + 1), 1)] = jnp.zeros((1, species), jnp.float32)

    for axis in AXES:
        for side in (0, 1):
            clear(axis, side)

    def scale(step):
        return 0.2 if step == 0 else 0.05 if step == STEPS - 1 else 0.1

    def advance(step, k):
        p = step % 2
        start, count = span(k)

        @pl.loop(0, depth // 8)
        def _(tile):
            at = pl.multiple_of(PAD + tile * 8, 8)
            source = pl.multiple_of(tile * 8, 8)

            def cell(y, x, shift=0):
                return field[p][y, 1 + start + x, pl.ds(at + shift, 8)]

            before = [cell(y, -1) for y in range(1, rows + 1)]
            here = [cell(y, 0) for y in range(1, rows + 1)]
            for x in range(count):
                after = [cell(y, x + 1) for y in range(1, rows + 1)]
                column = [cell(0, x), *here, cell(rows + 1, x)]
                for y in range(rows):
                    here_y = here[y]
                    around = (before[y] + after[y]) + (column[y] + column[y + 2])
                    around = around + (cell(y + 1, x, -1) + cell(y + 1, x, 1))
                    bound = limit[y, start + x, pl.ds(source, 8)]
                    if step == 0:
                        bound = bound + bound
                    field[1 - p][y + 1, 1 + start + x, pl.ds(at, 8)] = scale(step) * (
                        around + here_y * (6.0 - bound * here_y))
                before, here = here, after

    def advance_edges(step, y):
        p = step % 2
        tiles = depth // 8
        group = next(g for g in (4, 3, 2, 1) if tiles % g == 0)

        @pl.loop(0, tiles // group)
        def _(block):
            for n in range(group):
                at = pl.multiple_of(PAD + block * (8 * group) + 8 * n, 8)
                source = pl.multiple_of(block * (8 * group) + 8 * n, 8)
                for edge in (0, 1):
                    start = edge * (width - EDGE)

                    def cell(x, shift=0, up=0):
                        return field[p][1 + y + up, 1 + start + x, pl.ds(at + shift, 8)]

                    line = [cell(x) for x in range(-1, EDGE + 1)]
                    for x in range(EDGE):
                        here = line[x + 1]
                        around = (line[x] + line[x + 2]) + (cell(x, 0, -1) + cell(x, 0, 1))
                        around = around + (cell(x, -1) + cell(x, 1))
                        bound = limit[y, start + x, pl.ds(source, 8)]
                        if step == 0:
                            bound = bound + bound
                        field[1 - p][1 + y, 1 + start + x, pl.ds(at, 8)] = scale(step) * (
                            around + here * (6.0 - bound * here))

    def centre(step, k):
        p = step % 2
        if step == 0:
            load_limit(k).wait()
        by_side("rows", lambda side: y_face(1 - side, p, k, False, side).wait_recv())
        by_side("slabs", lambda side: z_face(1 - side, p, k, False, side).wait_recv())
        if step >= 1:
            by_side("rows", lambda side: y_face(side, 1 - p, k, False, side).wait_send())
            by_side("slabs", lambda side: z_face(side, 1 - p, k, False, side).wait_send())
        advance(step, k)
        if step < STEPS - 1:
            by_side("rows", lambda side: y_face(side, 1 - p, k, False, side).start())
            by_side("slabs", lambda side: z_face(side, 1 - p, k, False, side).start())

    def edges(step, j):
        p = step % 2
        y = row(j)
        group = j // half

        def at_row(side):
            return jnp.logical_and(has["rows", side], y == side * (rows - 1))

        for side in (0, 1):
            @pl.when(at_row(side))
            def _():
                for k in (0, last):
                    y_face(1 - side, p, k, False, side).wait_recv()
                    if step >= 1:
                        y_face(side, 1 - p, k, False, side).wait_send()

        @pl.when(lax.rem(j, half) == 0)
        def _():
            for edge in (0, 1):
                by_side("slabs", lambda side: e_face(1 - side, p, edge, group, False, side).wait_recv())
                if step >= 1:
                    by_side("slabs", lambda side: e_face(side, 1 - p, edge, group, False, side).wait_send())

        by_side("cols", lambda side: x_face(1 - side, step, j, False, side).wait_recv())
        if step >= 1:
            by_side("cols", lambda side: x_face(side, step - 1, j, False, side).wait_send())
        advance_edges(step, y)
        if step < STEPS - 1:
            for side in (0, 1):
                send_x(side, step + 1, j)
            for side in (0, 1):
                @pl.when(at_row(side))
                def _():
                    for k in (0, last):
                        y_face(side, 1 - p, k, False, side).start()

            @pl.when(lax.rem(j, half) == half - 1)
            def _():
                for edge in (0, 1):
                    by_side("slabs", lambda side: e_face(side, 1 - p, edge, group, False, side).start())

    forwards = {}
    if via:
        for event in range(STEPS):
            for n in range(share):
                j = first_relayed(event) + n
                when = (FIRST + n) if event == 0 else (event - 1) * slots + j + LATE
                forwards.setdefault(min(when, STEPS * slots - 1), []).append((event, j))

    for step in range(STEPS):
        if step == 0:
            for k in (0, last, 1):
                load_tracer(k).wait()

        @pl.loop(0, slots)
        def _(slot):
            if step == 0:
                for k in range(2, last):
                    pl.when(slot == k - 1)(functools.partial(lambda k: load_tracer(k).wait(), k))
                centre(step, slot + 1)

                @pl.when(slot == 0)
                def _():
                    for k in (0, last):
                        load_limit(k).wait()
            edges(step, slot)
            for n in range(slots):
                for event, j in forwards.get(step * slots + n, []):
                    pl.when(slot == n)(functools.partial(forward, event, j))
            if step > 0:
                centre(step, slot + 1)

    p = (STEPS - 1) % 2

    @pl.loop(1, last)
    def _(k):
        by_side("rows", lambda side: y_face(side, p, k, False, side).wait_send())
        by_side("slabs", lambda side: z_face(side, p, k, False, side).wait_send())

    for k in (0, last):
        by_side("rows", lambda side: y_face(side, p, k, False, side).wait_send())
        for group in range(rows // half):
            by_side("slabs", lambda side: e_face(side, p, k // last, group, False, side).wait_send())
    for j in range(rows):
        by_side("cols", lambda side: x_face(side, STEPS - 1, j, False, side).wait_send())
    for when in sorted(forwards):
        for event, j in forwards[when]:
            for source in (1, 2):
                pl.when(col == via[source])(lambda: second_hop(source, event, j).wait_send())


def relays(mesh):
    if mesh.shape["cols"] != 4:
        return None
    devices = mesh.devices.transpose([mesh.axis_names.index(axis) for axis in AXES])[0, :, 0]
    chips = [getattr(device, "coords", None) for device in devices]
    if any(chip is None for chip in chips):
        return None
    apart = sum(a != b for a, b in zip(chips[1], chips[2]))
    return VIA if apart > 1 else None


def solution(mesh):
    sizes = dict(mesh.shape)
    via = relays(mesh)

    def on_device(tracer, crowding):
        rows, width, depth, species = tracer.shape
        half = rows // 2 if rows % 2 == 0 else rows
        groups, share, parts = rows // half, max(1, rows // 2), rows + 2
        dma = pltpu.SemaphoreType.DMA
        padded = (rows + 2, width + 2, depth + 2 * PAD, species)
        cell_count = rows * width * depth * species
        ended = pl.pallas_call(
            functools.partial(kernel, sizes, via),
            out_shape=pltpu.VMEM(padded, jnp.float32),
            in_specs=[pl.BlockSpec(memory_space=pl.ANY)] * 2,
            out_specs=pl.BlockSpec(memory_space=pltpu.VMEM),
            scratch_shapes=[
                pltpu.VMEM(padded, jnp.float32),
                pltpu.VMEM(tracer.shape, jnp.float32),
                dma((2, parts)),
                dma((2, 2, parts)), dma((2, 2, parts)),
                dma((2, 2, parts)), dma((2, 2, parts)),
                dma((2, 2, 2, groups)), dma((2, 2, 2, groups)),
                dma((2, 2, rows)), dma((2, 2, rows)),
                pltpu.VMEM((STEPS, share, depth, species), jnp.float32),
                dma((STEPS, share)), dma((STEPS, share)),
            ],
            compiler_params=pltpu.CompilerParams(
                collective_id=0, has_side_effects=True, vmem_limit_bytes=VMEM_LIMIT),
        )(tracer, crowding)
        return pl.pallas_call(
            write,
            out_shape=jax.ShapeDtypeStruct(tracer.shape, jnp.float32),
            in_specs=[pl.BlockSpec(memory_space=pltpu.VMEM)],
            out_specs=pl.BlockSpec(memory_space=pl.ANY),
            scratch_shapes=[dma((rows,))],
            compiler_params=pltpu.CompilerParams(vmem_limit_bytes=1 << 20),
        )(ended)

    return jax.shard_map(
        on_device, mesh=mesh,
        in_specs=(P("rows", "cols", "slabs", None), P("rows", "cols", "slabs", None)),
        out_specs=P("rows", "cols", "slabs", None), check_vma=False)
```

time: 42.3 us -> 45.1 us (1.066)
  Pallas kernels: 42.1 us -> 45 us
    pallas_call x1, Pallas kernels: 37.4 us -> 40.2 us  [on_device(): pl.pallas_call(functools.partial(kernel, sizes, via), out_shape=pltpu.VME...]
where the time goes in v1:
time: 45.1 us; the launch traced here: 45 us
  Pallas kernels  45 us (100%)
    pallas_call x1, Pallas kernels, on_device(): pl.pallas_call(functools.partial(kernel, sizes, via), out_shape=pltpu.VME...  40.2 us
    pallas_call x1, Pallas kernels, on_device(): pl.pallas_call(write, out_shape=jax.ShapeDtypeStruct(tracer.shape, jnp.fl...  4.72 us

profile of v1, /device:TPU:0, one launch (start us, length us, event | category | flops | bytes accessed | tf_op | source)
XLA Modules:
  0.0 45.0 jit_solution(9348068724304061076)
XLA Ops:
  0.0 40.2 %shard_map.28.ended = f32[6,66,112,128]{3,2,1,0:T(8,128)S(1)} custom-call(f32[4,64,96,128]{3,2,1,0:T(8,128)} %tracer.1, f32[4,64,96,128]{3,2,1,0:T(8,128)} %crowding.1), custom_call_target="tpu_custom_call" | custom-call | tf_op jit(solution)/shard_map/pallas_call | solution.py:393
  40.3 4.7 %shard_map.29 = f32[4,64,96,128]{3,2,1,0:T(8,128)} custom-call(f32[6,66,112,128]{3,2,1,0:T(8,128)S(1)} %shard_map.28.ended), custom_call_target="tpu_custom_call" | custom-call | tf_op jit(solution)/shard_map/pallas_call | solution.py:412

commit v2 on v1

--- a/solution.py
+++ b/solution.py
@@ -100,7 +100,7 @@
                       x_send.at[p, side, j], x_recv.at[p, other, j])
 
     def first_relayed(event):
-        return 0 if event % 2 == 0 else rows - share
+        return 0 if event % 2 == 1 else rows - share
 
     def first_hop(source, event, j, from_input):
         side, n = 2 - source, j - first_relayed(event)
@@ -333,6 +333,8 @@
 
         @pl.loop(0, slots)
         def _(slot):
+            if step > 0:
+                centre(step, slot + 1)
             if step == 0:
                 for k in range(2, last):
                     pl.when(slot == k - 1)(functools.partial(lambda k: load_tracer(k).wait(), k))
@@ -342,12 +344,10 @@
                 def _():
                     for k in (0, last):
                         load_limit(k).wait()
-            edges(step, slot)
             for n in range(slots):
                 for event, j in forwards.get(step * slots + n, []):
                     pl.when(slot == n)(functools.partial(forward, event, j))
-            if step > 0:
-                centre(step, slot + 1)
+            edges(step, slot)
 
     p = (STEPS - 1) % 2
 

time: 45.1 us -> 40.2 us (0.89)
  Pallas kernels: 45 us -> 40.1 us
    pallas_call x1, Pallas kernels: 40.2 us -> 35.4 us  [on_device(): pl.pallas_call(functools.partial(kernel, sizes, via), out_shape=pltpu.VME...]
where the time goes in v2:
time: 40.2 us; the launch traced here: 40.1 us
  Pallas kernels  40.1 us (100%)
    pallas_call x1, Pallas kernels, on_device(): pl.pallas_call(functools.partial(kernel, sizes, via), out_shape=pltpu.VME...  35.4 us
    pallas_call x1, Pallas kernels, on_device(): pl.pallas_call(write, out_shape=jax.ShapeDtypeStruct(tracer.shape, jnp.fl...  4.72 us

profile of v2, /device:TPU:0, one launch (start us, length us, event | category | flops | bytes accessed | tf_op | source)
XLA Modules:
  0.0 40.1 jit_solution(18380199716709208061)
XLA Ops:
  0.0 35.4 %shard_map.28.ended = f32[6,66,112,128]{3,2,1,0:T(8,128)S(1)} custom-call(f32[4,64,96,128]{3,2,1,0:T(8,128)} %tracer.1, f32[4,64,96,128]{3,2,1,0:T(8,128)} %crowding.1), custom_call_target="tpu_custom_call" | custom-call | tf_op jit(solution)/shard_map/pallas_call | solution.py:393
  35.4 4.7 %shard_map.29 = f32[4,64,96,128]{3,2,1,0:T(8,128)} custom-call(f32[6,66,112,128]{3,2,1,0:T(8,128)S(1)} %shard_map.28.ended), custom_call_target="tpu_custom_call" | custom-call | tf_op jit(solution)/shard_map/pallas_call | solution.py:412

commit v3 on v2

--- a/solution.py
+++ b/solution.py
@@ -220,21 +220,23 @@
             def cell(y, x, shift=0):
                 return field[p][y, 1 + start + x, pl.ds(at + shift, 8)]
 
-            before = [cell(y, -1) for y in range(1, rows + 1)]
-            here = [cell(y, 0) for y in range(1, rows + 1)]
+            here = [cell(y, 0) for y in range(rows + 2)]
+            slant = [cell(y, -1) + here[y + 1] for y in range(1, rows + 1)]
             for x in range(count):
-                after = [cell(y, x + 1) for y in range(1, rows + 1)]
-                column = [cell(0, x), *here, cell(rows + 1, x)]
+                after = [None, *[cell(y, x + 1) for y in range(1, rows + 1)], None]
+                steep = [here[y] + after[y + 1] for y in range(rows)]
                 for y in range(rows):
-                    here_y = here[y]
-                    around = (before[y] + after[y]) + (column[y] + column[y + 2])
-                    around = around + (cell(y + 1, x, -1) + cell(y + 1, x, 1))
+                    here_y = here[y + 1]
+                    around = (slant[y] + steep[y]) + (cell(y + 1, x, -1) + cell(y + 1, x, 1))
                     bound = limit[y, start + x, pl.ds(source, 8)]
                     if step == 0:
                         bound = bound + bound
                     field[1 - p][y + 1, 1 + start + x, pl.ds(at, 8)] = scale(step) * (
                         around + here_y * (6.0 - bound * here_y))
-                before, here = here, after
+                if x < count - 1:
+                    after[0], after[-1] = cell(0, x + 1), cell(rows + 1, x + 1)
+                    slant = [*steep[1:], here[rows] + after[rows + 1]]
+                    here = after
 
     def advance_edges(step, y):
         p = step % 2

time: 40.2 us -> 39.6 us (0.985)
  Pallas kernels: 40.1 us -> 39.4 us
    pallas_call x1, Pallas kernels: 35.4 us -> 34.7 us  [on_device(): pl.pallas_call(functools.partial(kernel, sizes, via), out_shape=pltpu.VME...]
where the time goes in v3:
time: 39.6 us; the launch traced here: 39.4 us
  Pallas kernels  39.4 us (99%)
    pallas_call x1, Pallas kernels, on_device(): pl.pallas_call(functools.partial(kernel, sizes, via), out_shape=pltpu.VME...  34.7 us
    pallas_call x1, Pallas kernels, on_device(): pl.pallas_call(write, out_shape=jax.ShapeDtypeStruct(tracer.shape, jnp.fl...  4.72 us

profile of v3, /device:TPU:0, one launch (start us, length us, event | category | flops | bytes accessed | tf_op | source)
XLA Modules:
  0.0 39.4 jit_solution(16835376700506146940)
XLA Ops:
  0.0 34.7 %shard_map.28.ended = f32[6,66,112,128]{3,2,1,0:T(8,128)S(1)} custom-call(f32[4,64,96,128]{3,2,1,0:T(8,128)} %tracer.1, f32[4,64,96,128]{3,2,1,0:T(8,128)} %crowding.1), custom_call_target="tpu_custom_call" | custom-call | tf_op jit(solution)/shard_map/pallas_call | solution.py:395
  34.7 4.7 %shard_map.29 = f32[4,64,96,128]{3,2,1,0:T(8,128)} custom-call(f32[6,66,112,128]{3,2,1,0:T(8,128)S(1)} %shard_map.28.ended), custom_call_target="tpu_custom_call" | custom-call | tf_op jit(solution)/shard_map/pallas_call | solution.py:414

commit v4 on v2

--- a/solution.py
+++ b/solution.py
@@ -13,23 +13,77 @@
 LATE = 2
 FIRST = 0
 PAD = 8
-VMEM_LIMIT = 40 * 1024 * 1024
+TAIL = 2
+RING = 8
 MESH = pl.DeviceIdType.MESH
 AXES = ("rows", "cols", "slabs")
 
 
-def write(ended, out, store_sem):
+def scale(step):
+    return 0.2 if step == 0 else 0.05 if step == STEPS - 1 else 0.1
+
+
+def stencil(step, now, limit, rows, depth, start, count, store):
+    @pl.loop(0, depth // 8)
+    def _(tile):
+        source = pl.multiple_of(tile * 8, 8)
+        at = pl.multiple_of(PAD + tile * 8, 8)
+
+        def cell(y, x, shift=0):
+            return now[y, 1 + start + x, pl.ds(at + shift, 8)]
+
+        here = [cell(y, 0) for y in range(rows + 2)]
+        slant = [cell(y, -1) + here[y + 1] for y in range(1, rows + 1)]
+        for x in range(count):
+            after = [None, *[cell(y, x + 1) for y in range(1, rows + 1)], None]
+            steep = [here[y] + after[y + 1] for y in range(rows)]
+            for y in range(rows):
+                middle = here[y + 1]
+                around = (slant[y] + steep[y]) + (cell(y + 1, x, -1) + cell(y + 1, x, 1))
+                bound = limit[y, start + x, pl.ds(source, 8)]
+                if step == 0:
+                    bound = bound + bound
+                store(x, y, source, scale(step) * (around + middle * (6.0 - bound * middle)))
+            if x < count - 1:
+                after[0], after[-1] = cell(0, x + 1), cell(rows + 1, x + 1)
+                slant = [*steep[1:], here[rows] + after[rows + 1]]
+                here = after
+
+
+def tail_start(rows, width):
+    middle = (width - 2 * EDGE) // rows
+    return EDGE + (rows - TAIL) * middle
+
+
+def write(held, out, stage, store_sem, stage_sem):
     rows, width, depth, species = out.shape
-    copies = [pltpu.make_async_copy(
-        ended.at[1 + y, pl.ds(1, width), pl.ds(PAD, depth)], out.at[y], store_sem.at[y])
-        for y in range(rows)]
-    for copy in copies:
+    field = held.at[pl.ds(0, rows + 2)]
+    limit = held.at[pl.ds(rows + 2, rows), pl.ds(0, width), pl.ds(0, depth)]
+    first, end = tail_start(rows, width), width - EDGE
+    ready = [pltpu.make_async_copy(
+        limit.at[y, pl.ds(start, count)], out.at[y, pl.ds(start, count)], store_sem.at[y, n])
+        for n, (start, count) in enumerate(((0, first), (end, EDGE))) for y in range(rows)]
+    for copy in ready:
         copy.start()
-    for copy in copies:
+    slots, _, piece = stage.shape[:3]
+    copies = []
+    for n in range((end - first) // piece):
+        start, slot = first + n * piece, n % slots
+        if n >= slots:
+            copies[n - slots].wait()
+
+        def store(x, y, at, value):
+            stage[slot, y, x, pl.ds(at, 8)] = value
+
+        stencil(STEPS - 1, field, limit, rows, depth, start, piece, store)
+        copies.append(pltpu.make_async_copy(
+            stage.at[slot], out.at[:, pl.ds(start, piece)], stage_sem.at[n]))
+        copies[n].start()
+    for copy in [*ready, *copies[max(0, len(copies) - slots):]]:
         copy.wait()
 
 
-def kernel(sizes, via, tracer, crowding, ended, other_field, limit, load_sem,
+def kernel(sizes, via, tracer, crowding, held, even_field, load_sem,
            y_send, y_recv, z_send, z_recv, e_send, e_recv, x_send, x_recv,
            relayed, r_recv, f_send):
     rows, width, depth, species = tracer.shape
@@ -38,7 +92,9 @@
     last = slots + 1
     half = rows // 2 if rows % 2 == 0 else rows
     share = rows // 2
-    field = (ended, other_field)
+    odd_field = held.at[pl.ds(0, rows + 2)]
+    limit = held.at[pl.ds(rows + 2, rows), pl.ds(0, width), pl.ds(0, depth)]
+    field = (even_field, odd_field)
     place = {axis: lax.axis_index(axis) for axis in AXES}
     has = {(axis, side): (place[axis] > 0) if side == 0 else (place[axis] < sizes[axis] - 1)
            for axis in AXES for side in (0, 1)}
@@ -205,36 +261,17 @@
         for side in (0, 1):
             clear(axis, side)
 
-    def scale(step):
-        return 0.2 if step == 0 else 0.05 if step == STEPS - 1 else 0.1
-
     def advance(step, k):
         p = step % 2
         start, count = span(k)
 
-        @pl.loop(0, depth // 8)
-        def _(tile):
-            at = pl.multiple_of(PAD + tile * 8, 8)
-            source = pl.multiple_of(tile * 8, 8)
-
-            def cell(y, x, shift=0):
-                return field[p][y, 1 + start + x, pl.ds(at + shift, 8)]
-
-            before = [cell(y, -1) for y in range(1, rows + 1)]
-            here = [cell(y, 0) for y in range(1, rows + 1)]
-            for x in range(count):
-                after = [cell(y, x + 1) for y in range(1, rows + 1)]
-                column = [cell(0, x), *here, cell(rows + 1, x)]
-                for y in range(rows):
-                    here_y = here[y]
-                    around = (before[y] + after[y]) + (column[y] + column[y + 2])
-                    around = around + (cell(y + 1, x, -1) + cell(y + 1, x, 1))
-                    bound = limit[y, start + x, pl.ds(source, 8)]
-                    if step == 0:
-                        bound = bound + bound
-                    field[1 - p][y + 1, 1 + start + x, pl.ds(at, 8)] = scale(step) * (
-                        around + here_y * (6.0 - bound * here_y))
-                before, here = here, after
+        def store(x, y, at, value):
+            if step == STEPS - 1:
+                limit[y, start + x, pl.ds(at, 8)] = value
+            else:
+                field[1 - p][y + 1, 1 + start + x, pl.ds(PAD + at, 8)] = value
+
+        stencil(step, field[p], limit, rows, depth, start, count, store)
 
     def advance_edges(step, y):
         p = step % 2
@@ -260,8 +297,11 @@
                         bound = limit[y, start + x, pl.ds(source, 8)]
                         if step == 0:
                             bound = bound + bound
-                        field[1 - p][1 + y, 1 + start + x, pl.ds(at, 8)] = scale(step) * (
-                            around + here * (6.0 - bound * here))
+                        value = scale(step) * (around + here * (6.0 - bound * here))
+                        if step == STEPS - 1:
+                            limit[y, start + x, pl.ds(source, 8)] = value
+                        else:
+                            field[1 - p][1 + y, 1 + start + x, pl.ds(at, 8)] = value
 
     def centre(step, k):
         p = step % 2
@@ -272,7 +312,10 @@
         if step >= 1:
             by_side("rows", lambda side: y_face(side, 1 - p, k, False, side).wait_send())
             by_side("slabs", lambda side: z_face(side, 1 - p, k, False, side).wait_send())
-        advance(step, k)
+        if step == STEPS - 1:
+            pl.when(k <= slots - TAIL)(lambda: advance(step, k))
+        else:
+            advance(step, k)
         if step < STEPS - 1:
             by_side("rows", lambda side: y_face(side, 1 - p, k, False, side).start())
             by_side("slabs", lambda side: z_face(side, 1 - p, k, False, side).start())
@@ -389,15 +432,14 @@
         groups, share, parts = rows // half, max(1, rows // 2), rows + 2
         dma = pltpu.SemaphoreType.DMA
         padded = (rows + 2, width + 2, depth + 2 * PAD, species)
-        cell_count = rows * width * depth * species
-        ended = pl.pallas_call(
+        vmem = pl.BlockSpec(memory_space=pltpu.VMEM)
+        held = pl.pallas_call(
             functools.partial(kernel, sizes, via),
-            out_shape=pltpu.VMEM(padded, jnp.float32),
+            out_shape=pltpu.VMEM((2 * rows + 2, *padded[1:]), jnp.float32),
             in_specs=[pl.BlockSpec(memory_space=pl.ANY)] * 2,
-            out_specs=pl.BlockSpec(memory_space=pltpu.VMEM),
+            out_specs=vmem,
             scratch_shapes=[
                 pltpu.VMEM(padded, jnp.float32),
-                pltpu.VMEM(tracer.shape, jnp.float32),
                 dma((2, parts)),
                 dma((2, 2, parts)), dma((2, 2, parts)),
                 dma((2, 2, parts)), dma((2, 2, parts)),
@@ -407,16 +449,18 @@
                 dma((STEPS, share)), dma((STEPS, share)),
             ],
             compiler_params=pltpu.CompilerParams(
-                collective_id=0, has_side_effects=True, vmem_limit_bytes=VMEM_LIMIT),
+                collective_id=0, has_side_effects=True, vmem_limit_bytes=23 << 20),
         )(tracer, crowding)
+        piece = next(n for n in (5, 6, 4, 3, 2, 1) if (width - 2 * EDGE) // rows % n == 0)
         return pl.pallas_call(
             write,
             out_shape=jax.ShapeDtypeStruct(tracer.shape, jnp.float32),
-            in_specs=[pl.BlockSpec(memory_space=pltpu.VMEM)],
+            in_specs=[vmem],
             out_specs=pl.BlockSpec(memory_space=pl.ANY),
-            scratch_shapes=[dma((rows,))],
-            compiler_params=pltpu.CompilerParams(vmem_limit_bytes=1 << 20),
-        )(ended)
+            scratch_shapes=[pltpu.VMEM((RING, rows, piece, depth, species), jnp.float32),
+                            dma((rows, 2)), dma((max(1, width // piece),))],
+            compiler_params=pltpu.CompilerParams(vmem_limit_bytes=9 << 20),
+        )(held)
 
     return jax.shard_map(
         on_device, mesh=mesh,

time: 40.2 us -> 38.6 us (0.960)
  Pallas kernels: 40.1 us -> 38.4 us
    pallas_call x1, Pallas kernels: 35.4 us -> 33.7 us  [on_device(): pl.pallas_call(functools.partial(kernel, sizes, via), out_shape=pltpu.VME...]
where the time goes in v4:
time: 38.6 us; the launch traced here: 38.4 us
  Pallas kernels  38.4 us (99%)
    pallas_call x1, Pallas kernels, on_device(): pl.pallas_call(functools.partial(kernel, sizes, via), out_shape=pltpu.VME...  33.7 us
    pallas_call x1, Pallas kernels, on_device(): pl.pallas_call(write, out_shape=jax.ShapeDtypeStruct(tracer.shape, jnp.fl...  4.75 us

profile of v4, /device:TPU:0, one launch (start us, length us, event | category | flops | bytes accessed | tf_op | source)
XLA Modules:
  0.0 38.4 jit_solution(6939111103553561049)
XLA Ops:
  0.0 33.7 %shard_map.28.held = f32[10,66,112,128]{3,2,1,0:T(8,128)S(1)} custom-call(f32[4,64,96,128]{3,2,1,0:T(8,128)} %tracer.1, f32[4,64,96,128]{3,2,1,0:T(8,128)} %crowding.1), custom_call_target="tpu_custom_call" | custom-call | tf_op jit(solution)/shard_map/pallas_call | solution.py:436
  33.7 4.7 %shard_map.29 = f32[4,64,96,128]{3,2,1,0:T(8,128)} custom-call(f32[10,66,112,128]{3,2,1,0:T(8,128)S(1)} %shard_map.28.held), custom_call_target="tpu_custom_call" | custom-call | tf_op jit(solution)/shard_map/pallas_call | solution.py:455

commit v5 on v4

--- a/solution.py
+++ b/solution.py
@@ -10,7 +10,7 @@
 STEPS = 4
 EDGE = 2
 VIA = {1: 3, 2: 0}
-LATE = 2
+LATE = 1
 FIRST = 0
 PAD = 8
 TAIL = 2
@@ -183,6 +183,15 @@
         pl.when(jnp.logical_and(has["cols", side], jnp.logical_not(relay)))(
             lambda: x_face(side, event, j, from_input, side).start())
 
+    def send_both(event, j, from_input=False):
+        if not via:
+            for side in (0, 1):
+                send_x(side, event, j, from_input)
+            return
+        pl.when(col == 1)(lambda: send_x(1, event, j, from_input))
+        send_x(0, event, j, from_input)
+        pl.when(col != 1)(lambda: send_x(1, event, j, from_input))
+
     def forward(event, j):
         for source in (1, 2):
             @pl.when(col == via[source])
@@ -229,8 +238,7 @@
     pl.semaphore_wait(barrier, (1 if via else 0) + sum(jnp.where(has[key], 1, 0) for key in has))
 
     for j in range(rows):
-        for side in (0, 1):
-            send_x(side, 0, j, True)
+        send_both(0, j, True)
     for k in [1, 0, last, *range(2, last)]:
         by_side("rows", lambda side: y_face(side, 0, k, True, side).start())
         if k in (0, last):
@@ -348,8 +356,7 @@
             by_side("cols", lambda side: x_face(side, step - 1, j, False, side).wait_send())
         advance_edges(step, y)
         if step < STEPS - 1:
-            for side in (0, 1):
-                send_x(side, step + 1, j)
+            send_both(step + 1, j)
             for side in (0, 1):
                 @pl.when(at_row(side))
                 def _():

time: 38.6 us -> 38.3 us (level)
  no operation moved by 1% of the time
where the time goes in v5:
time: 38.3 us; the launch traced here: 38.2 us
  Pallas kernels  38.2 us (100%)
    pallas_call x1, Pallas kernels, on_device(): pl.pallas_call(functools.partial(kernel, sizes, via), out_shape=pltpu.VME...  33.4 us
    pallas_call x1, Pallas kernels, on_device(): pl.pallas_call(write, out_shape=jax.ShapeDtypeStruct(tracer.shape, jnp.fl...  4.75 us

profile of v5, /device:TPU:0, one launch (start us, length us, event | category | flops | bytes accessed | tf_op | source)
XLA Modules:
  0.0 38.2 jit_solution(1126946722320678254)
XLA Ops:
  0.0 33.4 %shard_map.28.held = f32[10,66,112,128]{3,2,1,0:T(8,128)S(1)} custom-call(f32[4,64,96,128]{3,2,1,0:T(8,128)} %tracer.1, f32[4,64,96,128]{3,2,1,0:T(8,128)} %crowding.1), custom_call_target="tpu_custom_call" | custom-call | tf_op jit(solution)/shard_map/pallas_call | solution.py:443
  33.4 4.7 %shard_map.29 = f32[4,64,96,128]{3,2,1,0:T(8,128)} custom-call(f32[10,66,112,128]{3,2,1,0:T(8,128)S(1)} %shard_map.28.held), custom_call_target="tpu_custom_call" | custom-call | tf_op jit(solution)/shard_map/pallas_call | solution.py:462

commit v6 on v5

--- a/solution.py
+++ b/solution.py
@@ -179,7 +179,8 @@
             return
         first = first_relayed(event)
         relay = jnp.logical_and(col == 2 - side, jnp.logical_and(j >= first, j < first + share))
-        pl.when(relay)(lambda: first_hop(2 - side, event, j, from_input).start())
+        if not from_input:
+            pl.when(relay)(lambda: first_hop(2 - side, event, j, from_input).start())
         pl.when(jnp.logical_and(has["cols", side], jnp.logical_not(relay)))(
             lambda: x_face(side, event, j, from_input, side).start())
 
@@ -237,6 +238,12 @@
         load_limit(k).start()
     pl.semaphore_wait(barrier, (1 if via else 0) + sum(jnp.where(has[key], 1, 0) for key in has))
 
+    if via:
+        for source in (1, 2):
+            @pl.when(col == source)
+            def _():
+                for n in range(share):
+                    first_hop(source, 0, first_relayed(0) + n, True).start()
     for j in range(rows):
         send_both(0, j, True)
     for k in [1, 0, last, *range(2, last)]:

time: 38.3 us -> 38.4 us (level)
  no operation moved by 1% of the time
where the time goes in v6:
time: 38.4 us; the launch traced here: 38.2 us
  Pallas kernels  38.2 us (99%)
    pallas_call x1, Pallas kernels, on_device(): pl.pallas_call(functools.partial(kernel, sizes, via), out_shape=pltpu.VME...  33.5 us
    pallas_call x1, Pallas kernels, on_device(): pl.pallas_call(write, out_shape=jax.ShapeDtypeStruct(tracer.shape, jnp.fl...  4.75 us

profile of v6, /device:TPU:0, one launch (start us, length us, event | category | flops | bytes accessed | tf_op | source)
XLA Modules:
  0.0 38.2 jit_solution(17713624297724560265)
XLA Ops:
  0.0 33.5 %shard_map.28.held = f32[10,66,112,128]{3,2,1,0:T(8,128)S(1)} custom-call(f32[4,64,96,128]{3,2,1,0:T(8,128)} %tracer.1, f32[4,64,96,128]{3,2,1,0:T(8,128)} %crowding.1), custom_call_target="tpu_custom_call" | custom-call | tf_op jit(solution)/shard_map/pallas_call | solution.py:450
  33.5 4.7 %shard_map.29 = f32[4,64,96,128]{3,2,1,0:T(8,128)} custom-call(f32[10,66,112,128]{3,2,1,0:T(8,128)S(1)} %shard_map.28.held), custom_call_target="tpu_custom_call" | custom-call | tf_op jit(solution)/shard_map/pallas_call | solution.py:469
